TPU v7x, 256 devices: a whole 4x4x8 slice. The times are simulated.
256 devices in a mesh: rows: 16 (over x, y_hi, core), mp: 16 (over y_lo, z).
Axes of the slice: x: 4, y: 4 (y_hi: 2, y_lo: 2; y = y_hi * 2 + y_lo), z: 8, core: 2. Of those that a mesh axis runs over, the one named last changes fastest.
Arguments:
- tokens: bfloat16 [2048, 3584], P('rows', 'mp'), may hold values from -6 to 6
- modality: int32 [2048], replicated, may hold values from 0 to 1, as said below
- attn_gain: float32 [2, 3584], P(None, 'mp'), may hold values from 0.1 to 1.9
- ffn_gain: float32 [2, 3584], P(None, 'mp'), may hold values from 0.1 to 1.9
- w_query: bfloat16 [2, 3584, 2048], P(None, 'mp', 'rows'), may hold values from -4 to 4
- w_keyval: bfloat16 [2, 3584, 1024], P(None, 'mp', 'rows'), may hold values from -4 to 4
- w_out: bfloat16 [2, 2048, 3584], P(None, 'rows', 'mp'), may hold values from -0.125 to 0.125
- w_gate: bfloat16 [2, 3584, 9472], P(None, 'mp', 'rows'), may hold values from -0.09375 to 0.09375
- w_up: bfloat16 [2, 3584, 9472], P(None, 'mp', 'rows'), may hold values from -0.09375 to 0.09375
- w_down: bfloat16 [2, 9472, 3584], P(None, 'rows', 'mp'), may hold values from -0.0625 to 0.0625
Outputs:
- mixed: bfloat16 [2048, 3584], P('rows', 'mp')
Inputs may be any that keep to these rules, and one draw needn't show every extreme that they name: `modality`: constant over each aligned block of 128 positions.
All inputs are finite; a program needn't handle non-finite values.
Results may differ from a plain program's by a relative error of at most 0.024.
Values may be sent and summed in bfloat16 or wider, within the bound.
A program may use at most 64 MiB of HBM per device.

v0:
```python
import jax
import jax.numpy as jnp
from jax import lax
from jax.sharding import Mesh
from jax.sharding import PartitionSpec as P

D = 3584
HD = 128
KV = 4
HEADS = 16
MODAL_BLOCK = 128
MP = ("mp_0", "mp_1")
EPSILON = 1e-06


def from_everyone(value, axis):
    copies = jnp.broadcast_to(value, (lax.axis_size(axis), *value.shape))
    return lax.all_to_all(copies, axis, split_axis=0, concat_axis=0, tiled=True)


def over_copies(value, axis):
    everything = from_everyone(value, axis)
    return jnp.sum(everything, axis=0)


def laid_out(blocks, dim):
    shape = list(blocks.shape[1:])
    shape[dim] *= blocks.shape[0]
    return jnp.moveaxis(blocks, 0, dim).reshape(shape)


def gather_directly(value, axis, dim):
    return laid_out(from_everyone(value, axis), dim)


def cut_along(value, dim, peers):
    shape = value.shape
    blocks = value.reshape(*shape[:dim], peers, shape[dim] // peers, *shape[dim + 1 :])
    return jnp.moveaxis(blocks, dim, 0)


def sent_and_summed(value, axis, dim):
    blocks = cut_along(value, dim, lax.axis_size(axis))
    arrived = lax.all_to_all(blocks, axis, split_axis=0, concat_axis=0, tiled=True)
    return arrived.astype(jnp.float32).sum(axis=0)


def reduced_to_own(blocks, axes, sequence):
    inside = blocks.shape[1:]
    blocks = blocks.reshape(*(lax.axis_size(a) for a in axes), *inside)
    blocks = jnp.moveaxis(blocks, sequence, range(len(axes))).reshape(-1, *inside)
    for k in sequence:
        blocks = lax.psum_scatter(blocks, axes[k], scatter_dimension=0, tiled=True)
    return blocks[0]


def summed_rows_2(value, axes, sequence, dim):
    peers = lax.axis_size(axes)
    return reduced_to_own(cut_along(value, dim, peers), axes, sequence)


def tower_rows(matrix, weights, tower_ids):
    per_block = matrix.shape[0] // tower_ids.shape[0]
    token_towers = jnp.repeat(tower_ids, per_block)
    is_image = (token_towers == 1)[:, None]
    nothing = jnp.zeros((), matrix.dtype)
    text_rows = jnp.where(is_image, nothing, matrix)
    image_rows = jnp.where(is_image, matrix, nothing)
    text_part = jnp.dot(text_rows, weights[0], preferred_element_type=jnp.float32)
    image_part = jnp.dot(image_rows, weights[1], preferred_element_type=jnp.float32)
    return text_part + image_part


def block_towers(modality):
    return modality.reshape(-1, MODAL_BLOCK)[:, 0]


def scaled_rows(hidden, squares, gains, token_towers):
    inverse = lax.rsqrt(squares / D + EPSILON)
    chosen = jnp.where(token_towers[:, None] == 1, gains[1][None, :], gains[0][None, :])
    return (hidden * inverse[:, None] * chosen).astype(jnp.bfloat16)


def pick_group(matrix, head_group):
    key_part = lax.dynamic_slice_in_dim(matrix, head_group * HD, HD, 1)
    value_part = lax.dynamic_slice_in_dim(matrix, KV * HD + head_group * HD, HD, 1)
    return jnp.concatenate((key_part, value_part), axis=1)


def local(tokens, modality, attn_gain, ffn_gain, w_query, w_keyval, w_out, w_gate, w_up, w_down):
    row_count = tokens.shape[0]
    total_rows = row_count * lax.axis_size("rows")
    share_rows = total_rows // lax.axis_size(MP)
    row_index = lax.axis_index("rows")
    mp_index = lax.axis_index(MP)
    own_towers = lax.dynamic_slice_in_dim(modality, row_index * row_count, row_count)
    hidden = tokens.astype(jnp.float32)
    squares = over_copies(jnp.sum(hidden * hidden, axis=1), MP)
    normed = scaled_rows(hidden, squares, attn_gain, own_towers)
    normed_all = gather_directly(normed, "rows", 0)
    joint_weight = jnp.concatenate((w_query, w_keyval), axis=2)
    picked = normed_all
    projected = sent_and_summed(
        tower_rows(picked, joint_weight, block_towers(modality)).astype(jnp.bfloat16), MP, 0
    ).astype(jnp.bfloat16)
    query_width = w_query.shape[2]
    heads_here = query_width // HD
    queries = projected[:, :query_width].reshape(share_rows, heads_here, HD)
    keyval_local = projected[:, query_width:]
    head_group = row_index * heads_here // (HEADS // KV)
    keyval_block = gather_directly(keyval_local, "rows", 1)
    keyval_all = gather_directly(pick_group(keyval_block, head_group), MP, 0)
    scores = jnp.einsum(
        "qhd,kd->hqk", queries, keyval_all[:, :HD], preferred_element_type=jnp.float32
    ) * HD ** (-0.5)
    query_pos = mp_index * share_rows + jnp.arange(share_rows, dtype=jnp.int32)
    key_pos = jnp.arange(total_rows, dtype=jnp.int32)
    allowed = key_pos[None, :] <= query_pos[:, None]
    scores = jnp.where(allowed[None, :, :], scores, -1e30)
    largest = jnp.max(scores, axis=2, keepdims=True)
    powers = jnp.exp(scores - largest)
    probs = (powers / jnp.sum(powers, axis=2, keepdims=True)).astype(jnp.bfloat16)
    context = jnp.einsum(
        "hqk,kd->qhd", probs, keyval_all[:, HD:], preferred_element_type=jnp.float32
    )
    context = context.astype(jnp.bfloat16).reshape(share_rows, query_width)
    context_all = gather_directly(context, MP, 0)
    picked = context_all
    residual = hidden + sent_and_summed(
        tower_rows(picked, w_out, block_towers(modality)).astype(jnp.bfloat16), "rows", 0
    )
    squares_ffn = over_copies(jnp.sum(residual * residual, axis=1), MP)
    normed_ffn = scaled_rows(residual, squares_ffn, ffn_gain, own_towers)
    normed_ffn_all = gather_directly(normed_ffn, "rows", 0)
    pair_weight = jnp.concatenate((w_gate, w_up), axis=2)
    hidden_width = w_gate.shape[2]
    picked = normed_ffn_all
    summed = summed_rows_2(
        tower_rows(picked, pair_weight, block_towers(modality)).astype(jnp.bfloat16), MP, (1, 0), 0
    ).astype(jnp.float32)
    activated = (jax.nn.silu(summed[:, :hidden_width]) * summed[:, hidden_width:]).astype(
        jnp.bfloat16
    )
    activated_all = lax.all_gather(activated, MP, axis=0, tiled=True)
    picked = activated_all
    mixed = residual + sent_and_summed(
        tower_rows(picked, w_down, block_towers(modality)).astype(jnp.bfloat16), "rows", 0
    )
    return mixed.astype(jnp.bfloat16)


def solution(mesh):
    torus = Mesh(mesh.devices.reshape(mesh.shape["rows"], 2, 8), ("rows", "mp_0", "mp_1"))
    in_specs = (
        P("rows", MP),
        P(),
        P(None, MP),
        P(None, MP),
        P(None, MP, "rows"),
        P(None, MP, "rows"),
        P(None, "rows", MP),
        P(None, MP, "rows"),
        P(None, MP, "rows"),
        P(None, "rows", MP),
    )
    out_specs = P("rows", MP)
    return jax.shard_map(local, mesh=torus, in_specs=in_specs, out_specs=out_specs, check_vma=False)
```

profile of v0, /device:TPU:1, one launch (start us, length us, event | category | flops | bytes accessed | tf_op | source)
XLA Modules:
  0.0 395.8 jit_solution(9332766273389813539)
XLA Ops:
  6.5 0.9 fusion.44
  7.4 0.6 broadcast_in_dim.161
  8.0 10.1 %all-to-all-start = ((f32[16,1,128]{2,1,0:T(1,128)}), f32[16,1,128]{2,1,0:T(1,128)S(1)}, u32[]{:S(2)}, u32[]{:S(2)}) async-start(f32[16,1,128]{2,1,0:T(1,128)} %broadcast_in_dim.161), calls=%async_computation | async-start | bytes 16384 | tf_op jit(solution)/shard_map/all_to_all | solution.py:18
  18.2 0.8 fusion.66
  18.9 0.8 dynamic-slice_compare_fusion
  19.7 5.7 %all-to-all-done = f32[16,1,128]{2,1,0:T(1,128)S(1)} async-done(((f32[16,1,128]{2,1,0:T(1,128)}), f32[16,1,128]{2,1,0:T(1,128)S(1)}, u32[]{:S(2)}, u32[]{:S(2)}) %all-to-all-start) | async-done | bytes 8224 | tf_op jit(solution)/shard_map/all_to_all | solution.py:18
  25.5 0.9 fusion.46
  26.4 1.1 broadcast_in_dim.167
  27.5 8.8 %all-to-all-start.1 = ((bf16[16,128,224]{1,2,0:T(8,128)(2,1)}), bf16[16,128,224]{1,2,0:T(8,128)(2,1)S(1)}, u32[]{:S(2)}, u32[]{:S(2)}) async-start(bf16[16,128,224]{1,2,0:T(8,128)(2,1)} %broadcast_in_dim.167), calls=%async_computation.1 | async-start | bytes 1835008 | tf_op jit(solution)/shard_map/all_to_all | solution.py:18
  36.2 0.1 copy.58
  36.4 0.1 fusion.59
  36.5 15.1 %all-to-all-done.1 = bf16[16,128,224]{1,2,0:T(8,128)(2,1)S(1)} async-done(((bf16[16,128,224]{1,2,0:T(8,128)(2,1)}), bf16[16,128,224]{1,2,0:T(8,128)(2,1)S(1)}, u32[]{:S(2)}, u32[]{:S(2)}) %all-to-all-start.1) | async-done | bytes 917536 | tf_op jit(solution)/shard_map/all_to_all | solution.py:18
  51.6 0.2 select_bitcast_fusion.2
  51.8 0.4 fusion.27
  52.2 0.4 fusion.15
  52.6 0.2 copy.98
  52.8 22.3 %all_to_all.52 = bf16[16,128,192]{1,2,0:T(8,128)(2,1)S(1)} all-to-all(bf16[16,128,192]{1,2,0:T(8,128)(2,1)S(1)} %bitcast.107), channel_id=1, replica_groups=mesh['rows'=16,'mp_0'=2,'mp_1'=8] {'mp_0','mp_1'}, dimensions={0} | all-to-all | bytes 1572864 | tf_op jit(solution)/shard_map/all_to_all | solution.py:44
  75.1 0.1 reduce_sum.77
  75.2 0.7 broadcast_in_dim.168
  76.0 6.5 %all-to-all-start.3 = ((bf16[16,128,64]{1,2,0:T(8,128)(2,1)}), bf16[16,128,64]{1,2,0:T(8,128)(2,1)S(1)}, u32[]{:S(2)}, u32[]{:S(2)}) async-start(bf16[16,128,64]{1,2,0:T(8,128)(2,1)} %broadcast_in_dim.168), calls=%async_computation.3 | async-start | bytes 524288 | tf_op jit(solution)/shard_map/all_to_all | solution.py:18
  82.5 8.9 %all-to-all-done.3 = bf16[16,128,64]{1,2,0:T(8,128)(2,1)S(1)} async-done(((bf16[16,128,64]{1,2,0:T(8,128)(2,1)}), bf16[16,128,64]{1,2,0:T(8,128)(2,1)S(1)}, u32[]{:S(2)}, u32[]{:S(2)}) %all-to-all-start.3) | async-done | bytes 262176 | tf_op jit(solution)/shard_map/all_to_all | solution.py:18
  91.3 0.1 copy.61
  91.5 1.1 broadcast_in_dim.169
  92.5 4.1 %all-to-all-start.4 = ((bf16[16,128,256]{2,1,0:T(8,128)(2,1)}), bf16[16,128,256]{2,1,0:T(8,128)(2,1)S(1)}, u32[]{:S(2)}, u32[]{:S(2)}) async-start(bf16[16,128,256]{2,1,0:T(8,128)(2,1)} %broadcast_in_dim.169), calls=%async_computation.4 | async-start | bytes 2097152 | tf_op jit(solution)/shard_map/all_to_all | solution.py:18
  96.7 25.6 %all-to-all-done.4 = bf16[16,128,256]{2,1,0:T(8,128)(2,1)S(1)} async-done(((bf16[16,128,256]{2,1,0:T(8,128)(2,1)}), bf16[16,128,256]{2,1,0:T(8,128)(2,1)S(1)}, u32[]{:S(2)}, u32[]{:S(2)}) %all-to-all-start.4) | async-done | bytes 1048608 | tf_op jit(solution)/shard_map/all_to_all | solution.py:18
  122.3 0.4 fusion.68
  122.7 0.3 fusion.19
  123.0 0.4 fusion.18
  123.4 0.1 copy.62
  123.5 0.1 broadcast_in_dim.171
  123.6 19.5 %all_to_all.53 = bf16[16,128,128]{2,1,0:T(8,128)(2,1)S(1)} all-to-all(bf16[16,128,128]{2,1,0:T(8,128)(2,1)S(1)} %broadcast_in_dim.171), channel_id=1, replica_groups=mesh['rows'=16,'mp_0'=2,'mp_1'=8] {'mp_0','mp_1'}, dimensions={0} | all-to-all | bytes 1048576 | tf_op jit(solution)/shard_map/all_to_all | solution.py:18
  143.1 0.1 broadcast_select_fusion
  143.3 0.4 fusion.54
  143.7 0.4 fusion.11
  144.1 0.2 copy.97
  144.3 21.5 %all_to_all.54 = bf16[16,128,224]{1,2,0:T(8,128)(2,1)S(1)} all-to-all(bf16[16,128,224]{1,2,0:T(8,128)(2,1)S(1)} %bitcast.105), channel_id=1, replica_groups=mesh['rows'=16,'mp_0'=2,'mp_1'=8] {'rows'}, dimensions={0} | all-to-all | bytes 1835008 | tf_op jit(solution)/shard_map/all_to_all | solution.py:44
  165.8 0.1 convert_reduce_fusion.1
  165.9 0.1 multiply_reduce_fusion
  166.0 0.6 broadcast_in_dim.175
  166.6 4.2 %all-to-all-start.7 = ((f32[16,1,128]{2,1,0:T(1,128)}), f32[16,1,128]{2,1,0:T(1,128)S(1)}, u32[]{:S(2)}, u32[]{:S(2)}) async-start(f32[16,1,128]{2,1,0:T(1,128)} %broadcast_in_dim.175), calls=%async_computation.7 | async-start | bytes 16384 | tf_op jit(solution)/shard_map/all_to_all | solution.py:18
  170.7 0.0 reduce-scatter.3.cloned.1.call-start
  170.8 7.2 %all-to-all-done.7 = f32[16,1,128]{2,1,0:T(1,128)S(1)} async-done(((f32[16,1,128]{2,1,0:T(1,128)}), f32[16,1,128]{2,1,0:T(1,128)S(1)}, u32[]{:S(2)}, u32[]{:S(2)}) %all-to-all-start.7) | async-done | bytes 8224 | tf_op jit(solution)/shard_map/all_to_all | solution.py:18
  178.0 0.1 multiply_convert_fusion
  178.1 0.1 broadcast_in_dim.180
  178.3 20.8 %all_to_all.55 = bf16[16,128,224]{1,2,0:T(8,128)(2,1)S(1)} all-to-all(bf16[16,128,224]{1,2,0:T(8,128)(2,1)S(1)} %broadcast_in_dim.180), channel_id=1, replica_groups=mesh['rows'=16,'mp_0'=2,'mp_1'=8] {'rows'}, dimensions={0} | all-to-all | bytes 1835008 | tf_op jit(solution)/shard_map/all_to_all | solution.py:18
  199.1 0.2 select_bitcast_fusion
  199.3 0.9 copy-done
  200.1 0.2 copy-done.1
  200.3 1.7 fusion.22
  202.0 1.8 fusion.10
  203.7 1.6 copy.76
  205.4 3.4 copy.67
  208.9 53.6 %reduce-scatter.3.cloned.1.call-done = bf16[2,128,1184]{1,2,0:T(8,128)(2,1)} async-done(((bf16[16,128,1184]{1,2,0:T(8,128)(2,1)}), bf16[2,128,1184]{1,2,0:T(8,128)(2,1)}) %reduce-scatter.3.cloned.1.call-update) | async-done | bytes 606224 | tf_op jit(solution)/shard_map/reduce_scatter | solution.py:53
  262.5 21.6 %reduce-scatter.5.cloned.1.call-done = bf16[1,128,1184]{1,2,0:T(8,128)(2,1)} async-done(((bf16[2,128,1184]{1,2,0:T(8,128)(2,1)}), bf16[1,128,1184]{1,2,0:T(8,128)(2,1)}) %reduce-scatter.5.cloned.1.call-update) | async-done | bytes 303120 | tf_op jit(solution)/shard_map/reduce_scatter | solution.py:53
  284.2 1.0 bitcast_convert_fusion
  285.2 0.7 fusion.39
  285.9 0.1 broadcast_bitcast_fusion
  286.0 64.7 %all-gather.2.cloned.1.call-done = bf16[2048,592]{0,1:T(8,128)(2,1)} async-done(((bf16[128,592]{0,1:T(8,128)(2,1)}), bf16[2048,592]{0,1:T(8,128)(2,1)}) %all-gather.2.cloned.1.call-update) | async-done | bytes 2424848 | tf_op jit(solution)/shard_map/all_gather | solution.py:144
  350.8 2.7 fusion.5
  353.5 0.9 fusion.12
  354.4 0.2 copy.96
  354.6 33.9 %all_to_all.56 = bf16[16,128,224]{1,2,0:T(8,128)(2,1)S(1)} all-to-all(bf16[16,128,224]{1,2,0:T(8,128)(2,1)S(1)} %bitcast.106), channel_id=1, replica_groups=mesh['rows'=16,'mp_0'=2,'mp_1'=8] {'rows'}, dimensions={0} | all-to-all | bytes 1835008 | tf_op jit(solution)/shard_map/all_to_all | solution.py:44
  388.5 0.1 convert_reduce_fusion
  388.6 0.7 add_convert_fusion.1
  (32 shorter events, 0.3 us)
Async XLA Ops:
  6.5 29.8 %copy-start.6 = (s32[2048]{0:T(1024)S(1)}, s32[2048]{0:T(1024)}, u32[]{:S(2)}) copy-start(s32[2048]{0:T(1024)} %param.11) | copy-start | bytes 24580
  6.5 29.7 %copy-start.5 = (bf16[2,224,64]{1,2,0:T(8,128)(2,1)S(1)}, bf16[2,224,64]{1,2,0:T(8,128)(2,1)}, u32[]{:S(2)}) copy-start(bf16[2,224,64]{1,2,0:T(8,128)(2,1)} %param.15) | copy-start | bytes 172036
  8.0 17.4 %all-to-all-start = ((f32[16,1,128]{2,1,0:T(1,128)}), f32[16,1,128]{2,1,0:T(1,128)S(1)}, u32[]{:S(2)}, u32[]{:S(2)}) async-start(f32[16,1,128]{2,1,0:T(1,128)} %broadcast_in_dim.161), calls=%async_computation | async-start | bytes 16384 | tf_op jit(solution)/shard_map/all_to_all | solution.py:18
  27.5 24.1 %all-to-all-start.1 = ((bf16[16,128,224]{1,2,0:T(8,128)(2,1)}), bf16[16,128,224]{1,2,0:T(8,128)(2,1)S(1)}, u32[]{:S(2)}, u32[]{:S(2)}) async-start(bf16[16,128,224]{1,2,0:T(8,128)(2,1)} %broadcast_in_dim.167), calls=%async_computation.1 | async-start | bytes 1835008 | tf_op jit(solution)/shard_map/all_to_all | solution.py:18
  36.2 15.6 %copy-start.3 = (bf16[2,224,128]{2,1,0:T(8,128)(2,1)S(1)}, bf16[2,224,128]{2,1,0:T(8,128)(2,1)}, u32[]{:S(2)}) copy-start(bf16[2,224,128]{2,1,0:T(8,128)(2,1)} %param.14) | copy-start | bytes 344068
  76.0 15.3 %all-to-all-start.3 = ((bf16[16,128,64]{1,2,0:T(8,128)(2,1)}), bf16[16,128,64]{1,2,0:T(8,128)(2,1)S(1)}, u32[]{:S(2)}, u32[]{:S(2)}) async-start(bf16[16,128,64]{1,2,0:T(8,128)(2,1)} %broadcast_in_dim.168), calls=%async_computation.3 | async-start | bytes 524288 | tf_op jit(solution)/shard_map/all_to_all | solution.py:18
  92.5 29.7 %all-to-all-start.4 = ((bf16[16,128,256]{2,1,0:T(8,128)(2,1)}), bf16[16,128,256]{2,1,0:T(8,128)(2,1)S(1)}, u32[]{:S(2)}, u32[]{:S(2)}) async-start(bf16[16,128,256]{2,1,0:T(8,128)(2,1)} %broadcast_in_dim.169), calls=%async_computation.4 | async-start | bytes 2097152 | tf_op jit(solution)/shard_map/all_to_all | solution.py:18
  123.4 19.9 %copy-start.4 = (bf16[2,128,224]{1,2,0:T(8,128)(2,1)S(1)}, bf16[2,128,224]{1,2,0:T(8,128)(2,1)}, u32[]{:S(2)}) copy-start(bf16[2,128,224]{1,2,0:T(8,128)(2,1)} %param.16) | copy-start | bytes 344068
  144.3 21.6 %copy-start.2 = (bf16[128,224]{0,1:T(8,128)(2,1)S(1)}, bf16[128,224]{0,1:T(8,128)(2,1)}, u32[]{:S(2)}) copy-start(bf16[128,224]{0,1:T(8,128)(2,1)} %param.10) | copy-start | bytes 172036
  144.3 26.5 %copy-start.7 = (f32[2,224]{1,0:T(2,128)S(1)}, f32[2,224]{1,0:T(2,128)}, u32[]{:S(2)}) copy-start(f32[2,224]{1,0:T(2,128)} %param.13) | copy-start | bytes 5380
  166.6 11.4 %all-to-all-start.7 = ((f32[16,1,128]{2,1,0:T(1,128)}), f32[16,1,128]{2,1,0:T(1,128)S(1)}, u32[]{:S(2)}, u32[]{:S(2)}) async-start(f32[16,1,128]{2,1,0:T(1,128)} %broadcast_in_dim.175), calls=%async_computation.7 | async-start | bytes 16384 | tf_op jit(solution)/shard_map/all_to_all | solution.py:18
  170.7 91.8 %reduce-scatter.3.cloned.1.call-start = ((), (), s32[]{:S(2)}) async-start(), calls=%async_computation.12 | async-start | bytes 5455872 | tf_op jit(solution)/shard_map/reduce_scatter | solution.py:53
  199.1 1.1 copy-start
  199.1 1.2 copy-start.1
  208.8 142.0 %copy-start.9 = (bf16[2,592,224]{1,2,0:T(8,128)(2,1)S(1)}, bf16[2,592,224]{1,2,0:T(8,128)(2,1)}, u32[]{:S(2)}) copy-start(bf16[2,592,224]{1,2,0:T(8,128)(2,1)} %param.19) | copy-start | bytes 1591300
  208.8 75.4 %reduce-scatter.5.cloned.1.call-start = ((), (), s32[]{:S(2)}) async-start(), calls=%async_computation.13 | async-start | bytes 909312 | tf_op jit(solution)/shard_map/reduce_scatter | solution.py:53
  262.5 88.3 %all-gather.2.cloned.1.call-start = ((), (), s32[]{:S(2)}) async-start(), calls=%async_computation.14 | async-start | bytes 2576384 | tf_op jit(solution)/shard_map/all_gather | solution.py:144
  350.8 2.7 copy-start.8
Sparse Core Ops, SparseCore 0:
  208.9 53.5 reduce-scatter.2
  265.0 19.1 reduce-scatter.4
  286.1 64.6 all-gather.1
where the time goes:
time: 397 us; the launch traced here: 396 us
  waiting for transfers between devices  202 us (51%)
  blocking collectives  118 us (30%)
  starting transfers between devices  33.8 us (9%)
  between operations  13.4 us (3%)
  local copies, waits for them, and re-layouts  12.1 us (3%)
  matrix products  9.47 us (2%)
  other arithmetic  6.53 us (2%)
    all_to_all x3, blocking collectives, sent_and_summed(): lax.all_to_all(blocks, axis, split_axis=0, concat_axis=0, tiled=True)  77.6 us
    reduce_scatter x2, waiting for transfers between devices, reduced_to_own(): blocks = lax.psum_scatter(blocks, axes[k], scatter_dimension=0, tiled=True)  75.2 us
    all_gather x1, waiting for transfers between devices, local(): activated_all = lax.all_gather(activated, MP, axis=0, tiled=True)  64.7 us
    all_to_all x5, waiting for transfers between devices, from_everyone(): return lax.all_to_all(copies, axis, split_axis=0, concat_axis=0, tiled=True)  62.4 us
    all_to_all x2, blocking collectives, from_everyone(): return lax.all_to_all(copies, axis, split_axis=0, concat_axis=0, tiled=True)  40.3 us
    all_to_all x5, starting transfers between devices, from_everyone(): return lax.all_to_all(copies, axis, split_axis=0, concat_axis=0, tiled=True)  33.6 us
  transfers between devices with their start and end apart: 8, of which 8 were waited for; matrix products, arithmetic and copies ran while one was open for 0% of the time, Pallas kernels for 0%

commit v1 on v0

--- a/solution.py
+++ b/solution.py
@@ -141,7 +141,9 @@
     activated = (jax.nn.silu(summed[:, :hidden_width]) * summed[:, hidden_width:]).astype(
         jnp.bfloat16
     )
-    activated_all = lax.all_gather(activated, MP, axis=0, tiled=True)
+    activated_all = jnp.concatenate(
+        lax.all_to_all(jnp.stack([activated] * lax.axis_size(MP)), MP, 0, 0), axis=0
+    )
     picked = activated_all
     mixed = residual + sent_and_summed(
         tower_rows(picked, w_down, block_towers(modality)).astype(jnp.bfloat16), "rows", 0

time: 397 us -> 383 us (0.965)
  waiting for transfers between devices: 202 us -> 138 us
  blocking collectives: 118 us -> 170 us
    all_gather x1 -> x0, waiting for transfers between devices: 64.7 us -> none  [local(): activated_all = lax.all_gather(activated, MP, axis=0, tiled=True)]
    all_to_all x0 -> x1, blocking collectives: none -> 61.2 us  [local(): lax.all_to_all(jnp.stack([activated] * lax.axis_size(MP)), MP, 0, 0)]
    all_to_all x3, blocking collectives: 77.6 us -> 68.6 us  [sent_and_summed(): lax.all_to_all(blocks, axis, split_axis=0, concat_axis=0, tiled=True)]
  transfers between devices with their start and end apart: 8 -> 7, of which waited for: 8 -> 7; matrix products, arithmetic and copies ran while one was open for 0% -> 0% of each run, Pallas kernels for 0% -> 0%
where the time goes in v1:
time: 383 us; the launch traced here: 382 us
  blocking collectives  170 us (44%)
  waiting for transfers between devices  138 us (36%)
  starting transfers between devices  33.7 us (9%)
  between operations  13.7 us (4%)
  local copies, waits for them, and re-layouts  13 us (3%)
  matrix products  7.66 us (2%)
  other arithmetic  6.26 us (2%)
    reduce_scatter x2, waiting for transfers between devices, reduced_to_own(): blocks = lax.psum_scatter(blocks, axes[k], scatter_dimension=0, tiled=True)  75.3 us
    all_to_all x3, blocking collectives, sent_and_summed(): lax.all_to_all(blocks, axis, split_axis=0, concat_axis=0, tiled=True)  68.6 us
    all_to_all x5, waiting for transfers between devices, from_everyone(): return lax.all_to_all(copies, axis, split_axis=0, concat_axis=0, tiled=True)  62.4 us
    all_to_all x1, blocking collectives, local(): lax.all_to_all(jnp.stack([activated] * lax.axis_size(MP)), MP, 0, 0)  61.2 us
    all_to_all x2, blocking collectives, from_everyone(): return lax.all_to_all(copies, axis, split_axis=0, concat_axis=0, tiled=True)  40.3 us
    all_to_all x5, starting transfers between devices, from_everyone(): return lax.all_to_all(copies, axis, split_axis=0, concat_axis=0, tiled=True)  33.7 us
  transfers between devices with their start and end apart: 7, of which 7 were waited for; matrix products, arithmetic and copies ran while one was open for 0% of the time, Pallas kernels for 0%

profile of v1, /device:TPU:1, one launch (start us, length us, event | category | flops | bytes accessed | tf_op | source)
XLA Modules:
  0.0 382.4 jit_solution(16232265211774221261)
XLA Ops:
  6.5 0.9 fusion.42
  7.4 0.6 broadcast_in_dim.159
  8.0 10.1 %all-to-all-start = ((f32[16,1,128]{2,1,0:T(1,128)}), f32[16,1,128]{2,1,0:T(1,128)S(1)}, u32[]{:S(2)}, u32[]{:S(2)}) async-start(f32[16,1,128]{2,1,0:T(1,128)} %broadcast_in_dim.159), calls=%async_computation | async-start | bytes 16384 | tf_op jit(solution)/shard_map/all_to_all | solution.py:18
  18.2 0.8 fusion.62
  18.9 0.8 dynamic-slice_compare_fusion
  19.7 5.7 %all-to-all-done = f32[16,1,128]{2,1,0:T(1,128)S(1)} async-done(((f32[16,1,128]{2,1,0:T(1,128)}), f32[16,1,128]{2,1,0:T(1,128)S(1)}, u32[]{:S(2)}, u32[]{:S(2)}) %all-to-all-start) | async-done | bytes 8224 | tf_op jit(solution)/shard_map/all_to_all | solution.py:18
  25.5 0.9 fusion.44
  26.4 1.0 broadcast_in_dim.165
  27.5 8.8 %all-to-all-start.1 = ((bf16[16,128,224]{1,2,0:T(8,128)(2,1)}), bf16[16,128,224]{1,2,0:T(8,128)(2,1)S(1)}, u32[]{:S(2)}, u32[]{:S(2)}) async-start(bf16[16,128,224]{1,2,0:T(8,128)(2,1)} %broadcast_in_dim.165), calls=%async_computation.1 | async-start | bytes 1835008 | tf_op jit(solution)/shard_map/all_to_all | solution.py:18
  36.2 0.1 copy.64
  36.4 0.1 fusion.57
  36.5 15.1 %all-to-all-done.1 = bf16[16,128,224]{1,2,0:T(8,128)(2,1)S(1)} async-done(((bf16[16,128,224]{1,2,0:T(8,128)(2,1)}), bf16[16,128,224]{1,2,0:T(8,128)(2,1)S(1)}, u32[]{:S(2)}, u32[]{:S(2)}) %all-to-all-start.1) | async-done | bytes 917536 | tf_op jit(solution)/shard_map/all_to_all | solution.py:18
  51.6 0.2 select_bitcast_fusion.4
  51.8 0.4 fusion.25
  52.2 0.4 fusion.15
  52.6 0.2 copy.118
  52.8 22.3 %all_to_all.57 = bf16[16,128,192]{1,2,0:T(8,128)(2,1)S(1)} all-to-all(bf16[16,128,192]{1,2,0:T(8,128)(2,1)S(1)} %bitcast.117), channel_id=1, replica_groups=mesh['rows'=16,'mp_0'=2,'mp_1'=8] {'mp_0','mp_1'}, dimensions={0} | all-to-all | bytes 1572864 | tf_op jit(solution)/shard_map/all_to_all | solution.py:44
  75.1 0.1 reduce_sum.77
  75.2 0.7 broadcast_in_dim.166
  76.0 6.5 %all-to-all-start.3 = ((bf16[16,128,64]{1,2,0:T(8,128)(2,1)}), bf16[16,128,64]{1,2,0:T(8,128)(2,1)S(1)}, u32[]{:S(2)}, u32[]{:S(2)}) async-start(bf16[16,128,64]{1,2,0:T(8,128)(2,1)} %broadcast_in_dim.166), calls=%async_computation.3 | async-start | bytes 524288 | tf_op jit(solution)/shard_map/all_to_all | solution.py:18
  82.5 8.9 %all-to-all-done.3 = bf16[16,128,64]{1,2,0:T(8,128)(2,1)S(1)} async-done(((bf16[16,128,64]{1,2,0:T(8,128)(2,1)}), bf16[16,128,64]{1,2,0:T(8,128)(2,1)S(1)}, u32[]{:S(2)}, u32[]{:S(2)}) %all-to-all-start.3) | async-done | bytes 262176 | tf_op jit(solution)/shard_map/all_to_all | solution.py:18
  91.4 0.1 copy.67
  91.5 1.1 broadcast_in_dim.167
  92.6 4.1 %all-to-all-start.4 = ((bf16[16,128,256]{2,1,0:T(8,128)(2,1)}), bf16[16,128,256]{2,1,0:T(8,128)(2,1)S(1)}, u32[]{:S(2)}, u32[]{:S(2)}) async-start(bf16[16,128,256]{2,1,0:T(8,128)(2,1)} %broadcast_in_dim.167), calls=%async_computation.4 | async-start | bytes 2097152 | tf_op jit(solution)/shard_map/all_to_all | solution.py:18
  96.7 25.6 %all-to-all-done.4 = bf16[16,128,256]{2,1,0:T(8,128)(2,1)S(1)} async-done(((bf16[16,128,256]{2,1,0:T(8,128)(2,1)}), bf16[16,128,256]{2,1,0:T(8,128)(2,1)S(1)}, u32[]{:S(2)}, u32[]{:S(2)}) %all-to-all-start.4) | async-done | bytes 1048608 | tf_op jit(solution)/shard_map/all_to_all | solution.py:18
  122.3 0.4 fusion.64
  122.7 0.3 fusion.17
  123.0 0.4 fusion.16
  123.4 0.1 copy.68
  123.5 0.1 broadcast_in_dim.169
  123.6 19.5 %all_to_all.58 = bf16[16,128,128]{2,1,0:T(8,128)(2,1)S(1)} all-to-all(bf16[16,128,128]{2,1,0:T(8,128)(2,1)S(1)} %broadcast_in_dim.169), channel_id=1, replica_groups=mesh['rows'=16,'mp_0'=2,'mp_1'=8] {'mp_0','mp_1'}, dimensions={0} | all-to-all | bytes 1048576 | tf_op jit(solution)/shard_map/all_to_all | solution.py:18
  143.1 0.1 broadcast_select_fusion
  143.3 0.4 fusion.52
  143.7 0.4 fusion.14
  144.1 0.2 copy.117
  144.3 21.5 %all_to_all.59 = bf16[16,128,224]{1,2,0:T(8,128)(2,1)S(1)} all-to-all(bf16[16,128,224]{1,2,0:T(8,128)(2,1)S(1)} %bitcast.115), channel_id=1, replica_groups=mesh['rows'=16,'mp_0'=2,'mp_1'=8] {'rows'}, dimensions={0} | all-to-all | bytes 1835008 | tf_op jit(solution)/shard_map/all_to_all | solution.py:44
  165.8 0.1 convert_reduce_fusion.1
  165.9 0.6 broadcast_in_dim.172
  166.6 4.2 %all-to-all-start.7 = ((f32[16,1,128]{2,1,0:T(1,128)}), f32[16,1,128]{2,1,0:T(1,128)S(1)}, u32[]{:S(2)}, u32[]{:S(2)}) async-start(f32[16,1,128]{2,1,0:T(1,128)} %broadcast_in_dim.172), calls=%async_computation.7 | async-start | bytes 16384 | tf_op jit(solution)/shard_map/all_to_all | solution.py:18
  170.8 7.2 %all-to-all-done.7 = f32[16,1,128]{2,1,0:T(1,128)S(1)} async-done(((f32[16,1,128]{2,1,0:T(1,128)}), f32[16,1,128]{2,1,0:T(1,128)S(1)}, u32[]{:S(2)}, u32[]{:S(2)}) %all-to-all-start.7) | async-done | bytes 8224 | tf_op jit(solution)/shard_map/all_to_all | solution.py:18
  178.0 0.1 multiply_convert_fusion
  178.1 0.1 broadcast_in_dim.177
  178.3 20.8 %all_to_all.60 = bf16[16,128,224]{1,2,0:T(8,128)(2,1)S(1)} all-to-all(bf16[16,128,224]{1,2,0:T(8,128)(2,1)S(1)} %broadcast_in_dim.177), channel_id=1, replica_groups=mesh['rows'=16,'mp_0'=2,'mp_1'=8] {'rows'}, dimensions={0} | all-to-all | bytes 1835008 | tf_op jit(solution)/shard_map/all_to_all | solution.py:18
  199.1 0.2 select_bitcast_fusion.2
  199.3 0.9 copy-done
  200.1 0.2 copy-done.1
  200.3 1.7 fusion.20
  202.0 1.8 fusion.10
  203.8 1.6 copy.86
  205.4 3.4 copy.73
  208.9 53.6 %reduce-scatter.3.cloned.1.call-done = bf16[2,128,1184]{1,2,0:T(8,128)(2,1)} async-done(((bf16[16,128,1184]{1,2,0:T(8,128)(2,1)}), bf16[2,128,1184]{1,2,0:T(8,128)(2,1)}) %reduce-scatter.3.cloned.1.call-update) | async-done | bytes 606224 | tf_op jit(solution)/shard_map/reduce_scatter | solution.py:53
  262.5 21.7 %reduce-scatter.5.cloned.1.call-done = bf16[1,128,1184]{1,2,0:T(8,128)(2,1)} async-done(((bf16[2,128,1184]{1,2,0:T(8,128)(2,1)}), bf16[1,128,1184]{1,2,0:T(8,128)(2,1)}) %reduce-scatter.5.cloned.1.call-update) | async-done | bytes 303120 | tf_op jit(solution)/shard_map/reduce_scatter | solution.py:53
  284.2 1.0 bitcast_convert_fusion
  285.2 0.1 fusion.37
  285.3 0.3 stack.2
  285.6 61.2 %all_to_all.61 = bf16[16,128,592]{1,2,0:T(8,128)(2,1)S(1)} all-to-all(bf16[16,128,592]{1,2,0:T(8,128)(2,1)S(1)} %stack.2), channel_id=1, replica_groups=mesh['rows'=16,'mp_0'=2,'mp_1'=8] {'mp_0','mp_1'}, dimensions={0} | all-to-all | bytes 4849664 | tf_op jit(solution)/shard_map/all_to_all | solution.py:145
  346.9 0.4 select_bitcast_fusion
  347.3 0.7 copy-done.3
  347.9 0.9 fusion.6
  348.8 0.9 fusion.11
  349.7 0.2 copy.116
  349.9 24.9 %all_to_all.62 = bf16[16,128,224]{1,2,0:T(8,128)(2,1)S(1)} all-to-all(bf16[16,128,224]{1,2,0:T(8,128)(2,1)S(1)} %bitcast.116), channel_id=1, replica_groups=mesh['rows'=16,'mp_0'=2,'mp_1'=8] {'rows'}, dimensions={0} | all-to-all | bytes 1835008 | tf_op jit(solution)/shard_map/all_to_all | solution.py:44
  374.8 0.1 convert_reduce_fusion
  374.9 0.7 add_convert_fusion.1
  (29 shorter events, 0.3 us)
Async XLA Ops:
  6.5 29.8 %copy-start.7 = (s32[2048]{0:T(1024)S(1)}, s32[2048]{0:T(1024)}, u32[]{:S(2)}) copy-start(s32[2048]{0:T(1024)} %param.11) | copy-start | bytes 24580
  6.5 29.7 %copy-start.6 = (bf16[2,224,64]{1,2,0:T(8,128)(2,1)S(1)}, bf16[2,224,64]{1,2,0:T(8,128)(2,1)}, u32[]{:S(2)}) copy-start(bf16[2,224,64]{1,2,0:T(8,128)(2,1)} %param.15) | copy-start | bytes 172036
  8.0 17.4 %all-to-all-start = ((f32[16,1,128]{2,1,0:T(1,128)}), f32[16,1,128]{2,1,0:T(1,128)S(1)}, u32[]{:S(2)}, u32[]{:S(2)}) async-start(f32[16,1,128]{2,1,0:T(1,128)} %broadcast_in_dim.159), calls=%async_computation | async-start | bytes 16384 | tf_op jit(solution)/shard_map/all_to_all | solution.py:18
  27.5 24.1 %all-to-all-start.1 = ((bf16[16,128,224]{1,2,0:T(8,128)(2,1)}), bf16[16,128,224]{1,2,0:T(8,128)(2,1)S(1)}, u32[]{:S(2)}, u32[]{:S(2)}) async-start(bf16[16,128,224]{1,2,0:T(8,128)(2,1)} %broadcast_in_dim.165), calls=%async_computation.1 | async-start | bytes 1835008 | tf_op jit(solution)/shard_map/all_to_all | solution.py:18
  36.2 15.6 %copy-start.4 = (bf16[2,224,128]{2,1,0:T(8,128)(2,1)S(1)}, bf16[2,224,128]{2,1,0:T(8,128)(2,1)}, u32[]{:S(2)}) copy-start(bf16[2,224,128]{2,1,0:T(8,128)(2,1)} %param.14) | copy-start | bytes 344068
  76.0 15.4 %all-to-all-start.3 = ((bf16[16,128,64]{1,2,0:T(8,128)(2,1)}), bf16[16,128,64]{1,2,0:T(8,128)(2,1)S(1)}, u32[]{:S(2)}, u32[]{:S(2)}) async-start(bf16[16,128,64]{1,2,0:T(8,128)(2,1)} %broadcast_in_dim.166), calls=%async_computation.3 | async-start | bytes 524288 | tf_op jit(solution)/shard_map/all_to_all | solution.py:18
  92.6 29.7 %all-to-all-start.4 = ((bf16[16,128,256]{2,1,0:T(8,128)(2,1)}), bf16[16,128,256]{2,1,0:T(8,128)(2,1)S(1)}, u32[]{:S(2)}, u32[]{:S(2)}) async-start(bf16[16,128,256]{2,1,0:T(8,128)(2,1)} %broadcast_in_dim.167), calls=%async_computation.4 | async-start | bytes 2097152 | tf_op jit(solution)/shard_map/all_to_all | solution.py:18
  123.4 19.9 %copy-start.5 = (bf16[2,128,224]{1,2,0:T(8,128)(2,1)S(1)}, bf16[2,128,224]{1,2,0:T(8,128)(2,1)}, u32[]{:S(2)}) copy-start(bf16[2,128,224]{1,2,0:T(8,128)(2,1)} %param.16) | copy-start | bytes 344068
  144.3 21.6 %copy-start.2 = (bf16[128,224]{0,1:T(8,128)(2,1)S(1)}, bf16[128,224]{0,1:T(8,128)(2,1)}, u32[]{:S(2)}) copy-start(bf16[128,224]{0,1:T(8,128)(2,1)} %param.10) | copy-start | bytes 172036
  144.3 26.5 %copy-start.8 = (f32[2,224]{1,0:T(2,128)S(1)}, f32[2,224]{1,0:T(2,128)}, u32[]{:S(2)}) copy-start(f32[2,224]{1,0:T(2,128)} %param.13) | copy-start | bytes 5380
  166.6 11.4 %all-to-all-start.7 = ((f32[16,1,128]{2,1,0:T(1,128)}), f32[16,1,128]{2,1,0:T(1,128)S(1)}, u32[]{:S(2)}, u32[]{:S(2)}) async-start(f32[16,1,128]{2,1,0:T(1,128)} %broadcast_in_dim.172), calls=%async_computation.7 | async-start | bytes 16384 | tf_op jit(solution)/shard_map/all_to_all | solution.py:18
  170.7 91.8 %reduce-scatter.3.cloned.1.call-start = ((), (), s32[]{:S(2)}) async-start(), calls=%async_computation.13 | async-start | bytes 5455872 | tf_op jit(solution)/shard_map/reduce_scatter | solution.py:53
  199.1 1.1 copy-start
  199.1 1.2 copy-start.1
  208.8 75.4 %reduce-scatter.5.cloned.1.call-start = ((), (), s32[]{:S(2)}) async-start(), calls=%async_computation.14 | async-start | bytes 909312 | tf_op jit(solution)/shard_map/reduce_scatter | solution.py:53
  346.9 1.1 copy-start.3
Sparse Core Ops, SparseCore 0:
  208.9 53.5 reduce-scatter.2
  265.0 19.1 reduce-scatter.4
